TPU v7x, 32 devices: a whole 2x2x4 slice. The times are simulated.
32 devices in a mesh: row: 8 (over z, x), col: 4 (over y, core).
Axes of the slice: x: 2, y: 2, z: 4, core: 2. Of those that a mesh axis runs over, the one named last changes fastest.
Arguments:
- t2_amps: bfloat16 [16384, 49152], P('row', 'col'), may hold values from -0.5 to 0.5
- l2_amps: bfloat16 [256, 49152], P('row', 'col'), may hold values from -0.02734375 to 0.02734375
Outputs:
- ladder: bfloat16 [256, 49152], P('row', 'col')
All inputs are finite; a program needn't handle non-finite values.
Results may differ from a plain program's by a relative error of at most 0.0044.
Values may be sent and summed in bfloat16 or wider, within the bound.
A program may use at most 128 MiB of HBM per device.

v0:
```python
import jax
import jax.numpy as jnp
from jax import lax
from jax.sharding import PartitionSpec as P


def on_device(t2_amps, l2_amps):
    partial_value = jnp.dot(
        t2_amps,
        lax.all_gather(l2_amps, "row", axis=0, tiled=True).T,
        preferred_element_type=jnp.float32,
    )
    oooo = lax.psum(partial_value, "col")
    oooo_half = oooo.astype(jnp.bfloat16)
    ladder = lax.psum_scatter(
        lax.dot_general(
            oooo_half, t2_amps, (((0,), (0,)), ((), ())), preferred_element_type=jnp.float32
        ),
        "row",
        scatter_dimension=0,
        tiled=True,
    )
    return ladder.astype(jnp.bfloat16)


def solution(mesh):
    return jax.shard_map(
        on_device,
        mesh=mesh,
        in_specs=(P("row", "col"), P("row", "col")),
        out_specs=P("row", "col"),
        check_vma=False,
    )
```

profile of v0, /device:TPU:0, one launch (start us, length us, event | category | flops | bytes accessed | tf_op | source)
XLA Modules:
  0.0 413.1 jit_solution(6841744538810563476)
XLA Ops:
  6.5 0.0 all-gather.2.cloned.1.call-start
  6.5 0.7 all-gather.2.cloned.1.call-update
  7.3 0.0 reduce-scatter.2.cloned.1.call-start
  7.3 103.7 %all-gather.2.cloned.1.call-done = bf16[256,12288]{1,0:T(8,128)(2,1)} async-done(((bf16[32,12288]{1,0:T(8,128)(2,1)}), bf16[256,12288]{1,0:T(8,128)(2,1)}) %all-gather.2.cloned.1.call-update) | async-done | bytes 6291472 | tf_op jit(solution)/shard_map/all_gather | solution.py:10
  111.0 21.7 %fusion.2 = f32[2048,256]{1,0:T(8,128)S(1)} fusion(bf16[2048,12288]{1,0:T(8,128)(2,1)} %param.2, bf16[256,12288]{1,0:T(8,128)(2,1)} %all-gather.2.cloned.1.call-done), kind=kOutput, calls=%fused_computation.2 | convolution fusion | flops 12884901888 | bytes 58720256 | tf_op jit(solution)/shard_map/dot_general | solution.py:8
  132.6 40.2 %all-reduce.1 = bf16[2048,256]{1,0:T(8,128)(2,1)S(1)} all-reduce(f32[2048,256]{1,0:T(8,128)S(1)} %fusion.2), channel_id=1, replica_groups=mesh['row'=8,'col'=4] {'col'}, use_global_device_ids=true, to_apply=%region_0.0 | all-reduce | flops 524288 | bytes 3145728 | tf_op jit(solution)/shard_map/psum | solution.py:13
  172.8 24.8 %fusion.3 = f32[256,12288]{1,0:T(8,128)} fusion(bf16[2048,256]{1,0:T(8,128)(2,1)S(1)} %all-reduce.1, bf16[2048,12288]{1,0:T(8,128)(2,1)} %param.2), kind=kOutput, calls=%fused_computation.3 | convolution fusion | flops 12884901888 | bytes 63963136 | tf_op jit(solution)/shard_map/dot_general | solution.py:16
  197.6 0.0 reduce-scatter.2.cloned.1.call-update
  197.6 206.2 %reduce-scatter.2.cloned.1.call-done = f32[32,12288]{1,0:T(8,128)} async-done(((f32[256,12288]{1,0:T(8,128)}), f32[32,12288]{1,0:T(8,128)}) %reduce-scatter.2.cloned.1.call-update) | async-done | bytes 1572880 | tf_op jit(solution)/shard_map/reduce_scatter | solution.py:15
  403.9 2.4 convert_element_type.7
Async XLA Ops:
  6.5 104.4 %all-gather.2.cloned.1.call-start = ((), (), s32[]{:S(2)}) async-start(), calls=%async_computation.1 | async-start | bytes 7077888 | tf_op jit(solution)/shard_map/all_gather | solution.py:10
  7.3 396.6 %reduce-scatter.2.cloned.1.call-start = ((), (), s32[]{:S(2)}) async-start(), calls=%async_computation.2 | async-start | bytes 14155776 | tf_op jit(solution)/shard_map/reduce_scatter | solution.py:15
Sparse Core Ops, SparseCore 0:
  9.5 101.4 all-gather.1
  197.7 206.0 reduce-scatter.1
where the time goes:
time: 413 us
  waiting for transfers between devices  311 us (75%)
  matrix products  46.4 us (11%)
  blocking collectives  40.2 us (10%)
  between operations  13.4 us (3%)
    reduce_scatter x1, waiting for transfers between devices, on_device(): lax.psum_scatter(lax.dot_general(oooo_half, t2_amps, (((0,), (0,)), ((),...  206 us
    all_gather x1, waiting for transfers between devices, on_device(): lax.all_gather(l2_amps, 'row', axis=0, tiled=True)  104 us
    psum x1, blocking collectives, on_device(): oooo = lax.psum(partial_value, 'col')  40.2 us
    dot_general x1, matrix products, on_device(): lax.dot_general(oooo_half, t2_amps, (((0,), (0,)), ((), ())), preferred_e...  24.8 us
    dot_general x1, matrix products, on_device(): jnp.dot(t2_amps, lax.all_gather(l2_amps, 'row', axis=0, tiled=True).T, pr...  21.7 us
  transfers between devices with their start and end apart: 2, of which 2 were waited for; matrix products, arithmetic and copies ran while one was open for 0% of the time, Pallas kernels for 0%

commit v1 on v0

--- a/solution.py
+++ b/solution.py
@@ -10,7 +10,9 @@
         lax.all_gather(l2_amps, "row", axis=0, tiled=True).T,
         preferred_element_type=jnp.float32,
     )
-    oooo = lax.psum(partial_value, "col")
+    oooo = partial_value
+    for hop in (1, 2):
+        oooo = oooo + lax.ppermute(oooo, "col", [(dev, dev ^ hop) for dev in range(4)])
     oooo_half = oooo.astype(jnp.bfloat16)
     ladder = lax.psum_scatter(
         lax.dot_general(

time: 413 us -> 426 us (1.031)
  waiting for transfers between devices: 311 us -> 360 us
  blocking collectives: 40.2 us -> 0 us
    ppermute x0 -> x2, waiting for transfers between devices: none -> 50.3 us  [on_device(): lax.ppermute(oooo, 'col', [(dev, dev ^ hop) for dev in range(4)])]
    psum x1 -> x0, blocking collectives: 40.2 us -> none  [on_device(): oooo = lax.psum(partial_value, 'col')]
  transfers between devices with their start and end apart: 2 -> 4, of which waited for: 2 -> 4; matrix products, arithmetic and copies ran while one was open for 0% -> 0% of each run, Pallas kernels for 0% -> 0%
where the time goes in v1:
time: 426 us
  waiting for transfers between devices  360 us (85%)
  matrix products  47.8 us (11%)
  between operations  13.4 us (3%)
    reduce_scatter x1, waiting for transfers between devices, on_device(): lax.psum_scatter(lax.dot_general(oooo_half, t2_amps, (((0,), (0,)), ((),...  206 us
    all_gather x1, waiting for transfers between devices, on_device(): lax.all_gather(l2_amps, 'row', axis=0, tiled=True)  104 us
    ppermute x2, waiting for transfers between devices, on_device(): lax.ppermute(oooo, 'col', [(dev, dev ^ hop) for dev in range(4)])  50.3 us
    dot_general x1, matrix products, on_device(): lax.dot_general(oooo_half, t2_amps, (((0,), (0,)), ((), ())), preferred_e...  26.1 us
    dot_general x1, matrix products, on_device(): jnp.dot(t2_amps, lax.all_gather(l2_amps, 'row', axis=0, tiled=True).T, pr...  21.7 us
  transfers between devices with their start and end apart: 4, of which 4 were waited for; matrix products, arithmetic and copies ran while one was open for 0% of the time, Pallas kernels for 0%

profile of v1, /device:TPU:0, one launch (start us, length us, event | category | flops | bytes accessed | tf_op | source)
XLA Modules:
  0.0 426.0 jit_solution(7570361144645282699)
XLA Ops:
  6.5 0.0 all-gather.2.cloned.1.call-start
  6.5 0.7 all-gather.2.cloned.1.call-update
  7.3 0.0 reduce-scatter.2.cloned.1.call-start
  7.3 103.7 %all-gather.2.cloned.1.call-done = bf16[256,12288]{1,0:T(8,128)(2,1)} async-done(((bf16[32,12288]{1,0:T(8,128)(2,1)}), bf16[256,12288]{1,0:T(8,128)(2,1)}) %all-gather.2.cloned.1.call-update) | async-done | bytes 6291472 | tf_op jit(solution)/shard_map/all_gather | solution.py:10
  111.0 21.7 %fusion.1 = f32[2048,256]{1,0:T(8,128)S(1)} fusion(bf16[2048,12288]{1,0:T(8,128)(2,1)} %param.2, bf16[256,12288]{1,0:T(8,128)(2,1)} %all-gather.2.cloned.1.call-done), kind=kOutput, calls=%fused_computation.2 | convolution fusion | flops 12884901888 | bytes 58720256 | tf_op jit(solution)/shard_map/dot_general | solution.py:8
  132.6 0.1 collective-permute-start
  132.7 4.1 collective-permute-done
  136.9 0.3 add.8
  137.1 1.5 collective-permute-start.1
  138.7 46.2 %collective-permute-done.1 = f32[2048,256]{1,0:T(8,128)S(1)} collective-permute-done((f32[2048,256]{1,0:T(8,128)S(1)}, f32[2048,256]{1,0:T(8,128)S(1)}, u32[]{:S(2)}, u32[]{:S(2)}) %collective-permute-start.1) | collective-permute-done | bytes 2097184 | tf_op jit(solution)/shard_map/ppermute | solution.py:15
  184.9 26.1 %fusion = f32[256,12288]{1,0:T(8,128)} fusion(bf16[2048,12288]{1,0:T(8,128)(2,1)} %param.2, f32[2048,256]{1,0:T(8,128)S(1)} %add.8, f32[2048,256]{1,0:T(8,128)S(1)} %collective-permute-done.1), kind=kOutput, calls=%fused_computation.1 | convolution fusion | flops 12885950464 | bytes 67108864 | tf_op jit(solution)/shard_map/dot_general | solution.py:18
  211.0 0.0 reduce-scatter.2.cloned.1.call-update
  211.0 205.8 %reduce-scatter.2.cloned.1.call-done = f32[32,12288]{1,0:T(8,128)} async-done(((f32[256,12288]{1,0:T(8,128)}), f32[32,12288]{1,0:T(8,128)}) %reduce-scatter.2.cloned.1.call-update) | async-done | bytes 1572880 | tf_op jit(solution)/shard_map/reduce_scatter | solution.py:17
  416.8 2.4 convert_element_type.7
Async XLA Ops:
  6.5 104.4 %all-gather.2.cloned.1.call-start = ((), (), s32[]{:S(2)}) async-start(), calls=%async_computation.1 | async-start | bytes 7077888 | tf_op jit(solution)/shard_map/all_gather | solution.py:10
  7.3 409.5 %reduce-scatter.2.cloned.1.call-start = ((), (), s32[]{:S(2)}) async-start(), calls=%async_computation.2 | async-start | bytes 14155776 | tf_op jit(solution)/shard_map/reduce_scatter | solution.py:17
  132.6 4.2 collective-permute-start
  137.1 47.7 %collective-permute-start.1 = (f32[2048,256]{1,0:T(8,128)S(1)}, f32[2048,256]{1,0:T(8,128)S(1)}, u32[]{:S(2)}, u32[]{:S(2)}) collective-permute-start(f32[2048,256]{1,0:T(8,128)S(1)} %add.8), channel_id=1, source_target_pairs={{0,2},{1,3},{2,0},{3,1},{4,6},{5,7},{6,4},{7,5},{8,10},{9,11},{10,... | collective-permute-start | bytes 6291464 | tf_op jit(solution)/shard_map/ppermute | solution.py:15
Sparse Core Ops, SparseCore 0:
  9.5 101.4 all-gather.1
  211.1 205.6 reduce-scatter.1
